TPU v7x, 32 devices: a whole 2x2x4 slice. The times are simulated.
32 devices in a mesh: rep: 4 (over z), fsdp: 8 (over y, x, core).
Axes of the slice: x: 2, y: 2, z: 4, core: 2. Of those that a mesh axis runs over, the one named last changes fastest.
Arguments:
- hidden: bfloat16 [8192, 7168], P(('rep', 'fsdp')), may hold values from -6 to 6
- out_grad: bfloat16 [8192, 2048], P(('rep', 'fsdp')), may hold values from -0.125 to 0.125
- inner_params: float32 [4, 7168, 2048], P('rep', 'fsdp'), may hold values from -0.132 to 0.132
- first_moment: bfloat16 [4, 7168, 2048], P('rep', 'fsdp'), may hold values from -6 to 6
- second_moment: bfloat16 [4, 7168, 2048], P('rep', 'fsdp'), may hold values from 0.049804688 to 2
- outer_params: float32 [7168, 2048], P('fsdp', 'rep'), may hold values from -0.12 to 0.12
- outer_momentum: float32 [7168, 2048], P('fsdp', 'rep'), may hold values from -0.012 to 0.012
Outputs:
- new_params: float32 [7168, 2048], P('fsdp')
- new_momentum: float32 [7168, 2048], P('fsdp', 'rep')
- new_first: bfloat16 [4, 7168, 2048], P('rep', 'fsdp')
- new_second: bfloat16 [4, 7168, 2048], P('rep', 'fsdp')
All inputs are finite; a program needn't handle non-finite values.
Results may differ from a plain program's by a relative error of at most 0.009.
Values may be sent and summed in bfloat16 or wider, within the bound.
A program may use at most 192 MiB of HBM per device.

v0:
```python
import jax
import jax.numpy as jnp
from jax import lax
from jax.sharding import PartitionSpec as P

INNER_STEP = 500


beta_one = 0.9
beta_two = 0.95
epsilon = 1e-08
inner_rate = 0.0004
weight_decay = 0.1
outer_rate = 0.7
nesterov = 0.9


def per_device(
    hidden, out_grad, inner_params, first_moment, second_moment, outer_params, outer_momentum
):
    shard_rows = inner_params.shape[1]
    token_count = hidden.shape[0]
    columns = lax.all_to_all(hidden, "fsdp", split_axis=1, concat_axis=0, tiled=True)
    segment = lax.all_gather(out_grad, "fsdp", axis=0, tiled=True)
    blocks = segment.shape[0] // token_count
    partial_value = jnp.einsum(
        "btf,btd->bfd",
        columns.reshape(blocks, token_count, shard_rows),
        segment.reshape(blocks, token_count, segment.shape[1]),
        preferred_element_type=jnp.float32,
    )
    rounded = lax.optimization_barrier(partial_value.astype(jnp.bfloat16)).astype(jnp.float32)
    gradient = jnp.sum(rounded, axis=0)
    stacked = gradient[None]
    moment_one = beta_one * first_moment.astype(jnp.float32) + (1.0 - beta_one) * stacked
    moment_two = beta_two * second_moment.astype(jnp.float32) + (1.0 - beta_two) * stacked * stacked
    corrected_one = moment_one / (1.0 - beta_one**INNER_STEP)
    corrected_two = moment_two / (1.0 - beta_two**INNER_STEP)
    stepped = inner_params - inner_rate * (
        corrected_one / (jnp.sqrt(corrected_two) + epsilon) + weight_decay * inner_params
    )
    summed = lax.psum_scatter(stepped[0], "rep", scatter_dimension=1, tiled=True)
    outer_delta = outer_params - summed / lax.axis_size("rep")
    new_momentum = nesterov * outer_momentum + outer_delta
    updated = outer_params - outer_rate * (outer_delta + nesterov * new_momentum)
    gathered = lax.all_gather(updated, "rep", axis=1, tiled=True)
    return (
        gathered,
        new_momentum,
        moment_one.astype(jnp.bfloat16),
        moment_two.astype(jnp.bfloat16),
    )


def solution(mesh):
    return jax.shard_map(
        per_device,
        mesh=mesh,
        in_specs=(
            P(("rep", "fsdp"), None),
            P(("rep", "fsdp"), None),
            P("rep", "fsdp", None),
            P("rep", "fsdp", None),
            P("rep", "fsdp", None),
            P("fsdp", "rep"),
            P("fsdp", "rep"),
        ),
        out_specs=(
            P("fsdp", None),
            P("fsdp", "rep"),
            P("rep", "fsdp", None),
            P("rep", "fsdp", None),
        ),
        check_vma=False,
    )
```

profile of v0, /device:TPU:0, one launch (start us, length us, event | category | flops | bytes accessed | tf_op | source)
XLA Modules:
  0.0 421.4 jit_solution(17620051497730179171)
XLA Ops:
  7.2 0.0 all-gather.3.cloned.1.call-start
  7.2 0.7 all-gather.3.cloned.1.call-update
  7.9 0.0 reduce-scatter.2.cloned.1.call-start
  7.9 5.9 %copy.11 = bf16[256,7168]{0,1:T(8,128)(2,1)} copy(bf16[256,7168]{1,0:T(8,128)(2,1)} %param.7) | data formatting | bytes 7340032 | tf_op args[0]
  13.9 68.0 %all_to_all.16 = bf16[256,8,896]{0,2,1:T(8,128)(2,1)} all-to-all(bf16[256,8,896]{0,2,1:T(8,128)(2,1)} %bitcast.21), channel_id=1, replica_groups=mesh['rep'=4,'fsdp'=8] {'fsdp'}, dimensions={1} | all-to-all | bytes 7340032 | tf_op jit(solution)/shard_map/all_to_all | solution.py:23
  81.9 15.4 %all-gather.3.cloned.1.call-done = bf16[2048,2048]{1,0:T(8,128)(2,1)} async-done(((bf16[256,2048]{1,0:T(8,128)(2,1)}), bf16[2048,2048]{1,0:T(8,128)(2,1)}) %all-gather.3.cloned.1.call-update) | async-done | bytes 8388624 | tf_op jit(solution)/shard_map/all_gather | solution.py:24
  97.3 16.7 %convolution_convert_fusion = bf16[8,896,2048]{2,1,0:T(8,128)(2,1)} fusion(bf16[8,256,2048]{2,1,0:T(8,128)(2,1)} %bitcast.22, bf16[256,8,896]{0,2,1:T(8,128)(2,1)} %all_to_all.16), kind=kOutput, calls=%fused_computation.1 | convolution fusion | flops 7530872832 | bytes 41418752 | tf_op jit(solution)/shard_map/btf,btd->bfd/dot_general | solution.py:26
  114.0 13.6 %convert_reduce_fusion = f32[896,2048]{1,0:T(8,128)} fusion(bf16[8,896,2048]{2,1,0:T(8,128)(2,1)} %convolution_convert_fusion), kind=kLoop, calls=%fused_computation | loop fusion | flops 27525120 | bytes 36700160 | tf_op jit(solution)/shard_map/reduce_sum | solution.py:33
  127.6 13.6 %fusion.3 = (bf16[1,896,2048]{2,1,0:T(8,128)(2,1)}, f32[896,2048]{1,0:T(8,128)}, bf16[1,896,2048]{2,1,0:T(8,128)(2,1)}) fusion(f32[896,2048]{1,0:T(8,128)} %convert_reduce_fusion, bf16[1,896,2048]{2,1,0:T(8,128)(2,1)} %param.11, f32[1,896,2048]{2,1,0:T(8,128)} %param.9, bf16[1,896,2048]{2,1,0:T(8,128)(2,1)} %param.10), kind=kLoop, calls=%fused_computation.8 | loop fusion | flops 31195136 | bytes 36700160 | tf_op jit(solution)/shard_map/convert_element_type | solution.py:51
  141.2 0.0 copy-start
  141.2 0.0 reduce-scatter.2.cloned.1.call-update
  141.2 0.0 all-gather.5.cloned.1.call-start
  141.2 128.8 %reduce-scatter.2.cloned.1.call-done = f32[896,512]{1,0:T(8,128)} async-done(((f32[896,2048]{1,0:T(8,128)}), f32[896,512]{1,0:T(8,128)}) %reduce-scatter.2.cloned.1.call-update) | async-done | bytes 1835024 | tf_op jit(solution)/shard_map/reduce_scatter | solution.py:42
  270.0 0.0 copy-done
  270.0 4.6 %multiply_subtract_fusion = (f32[896,512]{1,0:T(8,128)}, f32[896,512]{1,0:T(8,128)}) fusion(f32[896,512]{1,0:T(8,128)S(1)} %copy-done, f32[896,512]{1,0:T(8,128)} %reduce-scatter.2.cloned.1.call-done, f32[896,512]{1,0:T(8,128)} %param.13), kind=kLoop, calls=%fused_computation.10 | loop fusion | flops 3670016 | bytes 9175040 | tf_op jit(solution)/shard_map/sub | solution.py:45
  274.6 0.0 all-gather.5.cloned.1.call-update
  274.6 133.1 %all-gather.5.cloned.1.call-done = f32[896,2048]{1,0:T(8,128)} async-done(((f32[896,512]{1,0:T(8,128)}), f32[896,2048]{1,0:T(8,128)}) %all-gather.5.cloned.1.call-update) | async-done | bytes 7340048 | tf_op jit(solution)/shard_map/all_gather | solution.py:46
  407.7 7.1 %copy.13 = f32[896,2048]{1,0:T(8,128)} copy(f32[896,2048]{1,0:T(8,128)} %all-gather.5.cloned.1.call-done) | data formatting | bytes 14680064
Async XLA Ops:
  7.2 90.1 %all-gather.3.cloned.1.call-start = ((), (), s32[]{:S(2)}) async-start(), calls=%async_computation.2 | async-start | bytes 9437184 | tf_op jit(solution)/shard_map/all_gather | solution.py:24
  7.9 262.1 %reduce-scatter.2.cloned.1.call-start = ((), (), s32[]{:S(2)}) async-start(), calls=%async_computation.3 | async-start | bytes 9175040 | tf_op jit(solution)/shard_map/reduce_scatter | solution.py:42
  141.2 128.8 %copy-start = (f32[896,512]{1,0:T(8,128)S(1)}, f32[896,512]{1,0:T(8,128)}, u32[]{:S(2)}) copy-start(f32[896,512]{1,0:T(8,128)} %param.12) | copy-start | bytes 5505028
  141.2 266.5 %all-gather.5.cloned.1.call-start = ((), (), s32[]{:S(2)}) async-start(), calls=%async_computation.4 | async-start | bytes 9175040 | tf_op jit(solution)/shard_map/all_gather | solution.py:46
Sparse Core Ops, SparseCore 0:
  9.9 87.3 all-gather.2
  141.3 128.6 reduce-scatter.1
  274.7 132.9 all-gather.4
where the time goes:
time: 422 us; the launch traced here: 421 us
  waiting for transfers between devices  278 us (66%)
  blocking collectives  68 us (16%)
  other arithmetic  31.8 us (8%)
  matrix products  16.7 us (4%)
  between operations  13.7 us (3%)
  local copies, waits for them, and re-layouts  13 us (3%)
    all_gather x1, waiting for transfers between devices, per_device(): gathered = lax.all_gather(updated, 'rep', axis=1, tiled=True)  133 us
    reduce_scatter x1, waiting for transfers between devices, per_device(): lax.psum_scatter(stepped[0], 'rep', scatter_dimension=1, tiled=True)  129 us
    all_to_all x1, blocking collectives, per_device(): lax.all_to_all(hidden, 'fsdp', split_axis=1, concat_axis=0, tiled=True)  68 us
    dot_general x1, matrix products, per_device(): jnp.einsum('btf,btd->bfd', columns.reshape(blocks, token_count, shard_row...  16.7 us
    all_gather x1, waiting for transfers between devices, per_device(): segment = lax.all_gather(out_grad, 'fsdp', axis=0, tiled=True)  15.4 us
    reduce_sum x1, other arithmetic, per_device(): gradient = jnp.sum(rounded, axis=0)  13.6 us
    convert_element_type x1, other arithmetic, per_device(): moment_two.astype(jnp.bfloat16)  13.6 us
    unnamed x4, local copies, waits for them, and re-layouts  13 us
  transfers between devices with their start and end apart: 3, of which 3 were waited for; matrix products, arithmetic and copies ran while one was open for 1% of the time, Pallas kernels for 0%

commit v1 on v0

v1 whole, which is shorter than its diff:
```python
import functools

import jax
import jax.numpy as jnp
from jax import lax
from jax.experimental import pallas as pl
from jax.experimental.pallas import tpu as pltpu
from jax.sharding import PartitionSpec as P

INNER_STEP = 500

beta_one = 0.9
beta_two = 0.95
epsilon = 1e-08
inner_rate = 0.0004
weight_decay = 0.1
outer_rate = 0.7
nesterov = 0.9

WIRE = jnp.bfloat16
WIRE_SCALE = 16.0
LAG_OWN = 2
LAG_FORWARD = 4


def encode(value):
    scaled = value * WIRE_SCALE
    square = scaled * scaled
    fourth = square * square
    eighth = fourth * fourth
    return jnp.where(scaled < 0.0, -eighth, eighth).astype(WIRE)


def decode(coded):
    wide = coded.astype(jnp.float32)
    root = jnp.sqrt(jnp.sqrt(jnp.sqrt(jnp.abs(wide)))) * (1.0 / WIRE_SCALE)
    return jnp.where(wide < 0.0, -root, root)


def outer_kernel(
    n, chunks, step_ref, outer_ref, mom_ref, out_ref, newmom_ref,
    from_left, from_right, acc, total,
    rs_send, rs_left, rs_right, ag_right, ag_left, ag_recv,
):
    z = lax.axis_index("rep")
    rows, block = outer_ref.shape
    rc = rows // chunks
    has_left, has_right = z > 0, z < n - 1

    barrier = pltpu.get_barrier_semaphore()

    @pl.when(has_left)
    def _():
        pl.semaphore_signal(barrier, inc=1, device_id={"rep": z - 1})

    @pl.when(has_right)
    def _():
        pl.semaphore_signal(barrier, inc=1, device_id={"rep": z + 1})

    pl.semaphore_wait(barrier, has_left.astype(jnp.int32) + has_right.astype(jnp.int32))

    def part(c, o):
        start = o * block
        if not isinstance(o, int):
            start = pl.multiple_of(start, 128)
        return pl.ds(pl.multiple_of(c * rc, rc), rc), pl.ds(start, block)

    def send_sum(src, c, o, to_right):
        at = part(c, o)
        return pltpu.make_async_remote_copy(
            src_ref=src.at[at],
            dst_ref=(from_left if to_right else from_right).at[at],
            send_sem=rs_send.at[c, o],
            recv_sem=(rs_left if to_right else rs_right).at[c, o],
            device_id={"rep": z + 1 if to_right else z - 1},
        )

    def send_new(c, o, to_right):
        at = part(c, o)
        return pltpu.make_async_remote_copy(
            src_ref=out_ref.at[at],
            dst_ref=out_ref.at[at],
            send_sem=(ag_right if to_right else ag_left).at[c, o],
            recv_sem=ag_recv.at[c, o],
            device_id={"rep": z + 1 if to_right else z - 1},
        )

    def wave(c, to_right):
        first = z == 0 if to_right else z == n - 1
        order = range(n - 1, 0, -1) if to_right else range(n - 1)
        for o in order:
            beyond = o > z if to_right else o < z
            at = part(c, o)

            @pl.when(jnp.logical_and(beyond, first))
            def _():
                acc[at] = encode(step_ref[at])
                send_sum(acc, c, o, to_right).start()

            @pl.when(jnp.logical_and(beyond, jnp.logical_not(first)))
            def _():
                send_sum(acc, c, o, to_right).wait_recv()
                came = (from_left if to_right else from_right)[at]
                acc[at] = encode(decode(came) + step_ref[at])
                send_sum(acc, c, o, to_right).start()

    def own(c):
        at = part(c, z)
        here = pl.ds(pl.multiple_of(c * rc, rc), rc)
        total[...] = step_ref[at]

        @pl.when(has_left)
        def _():
            send_sum(acc, c, z, True).wait_recv()
            total[...] += decode(from_left[at])

        @pl.when(has_right)
        def _():
            send_sum(acc, c, z, False).wait_recv()
            total[...] += decode(from_right[at])

        delta = outer_ref[here, :] - total[...] / n
        momentum = nesterov * mom_ref[here, :] + delta
        newmom_ref[here, :] = momentum
        updated = outer_ref[here, :] - outer_rate * (delta + nesterov * momentum)
        out_ref[at] = updated.astype(WIRE)

        @pl.when(has_right)
        def _():
            send_new(c, z, True).start()

        @pl.when(has_left)
        def _():
            send_new(c, z, False).start()

    def forward(c):
        for distance in range(1, n):
            for to_right in (True, False):
                o = z - distance if to_right else z + distance
                there = o >= 0 if to_right else o < n

                @pl.when(there)
                def _():
                    send_new(c, o, to_right).wait_recv()

                @pl.when(jnp.logical_and(there, has_right if to_right else has_left))
                def _():
                    send_new(c, o, to_right).start()

    def body(t, carry):
        @pl.when(t < chunks)
        def _():
            near_left = z < n // 2

            @pl.when(near_left)
            def _():
                wave(t, True)
                wave(t, False)

            @pl.when(jnp.logical_not(near_left))
            def _():
                wave(t, False)
                wave(t, True)

        @pl.when(jnp.logical_and(t >= LAG_OWN, t < chunks + LAG_OWN))
        def _():
            own(t - LAG_OWN)

        @pl.when(t >= LAG_FORWARD)
        def _():
            forward(t - LAG_FORWARD)

        return carry

    lax.fori_loop(0, chunks + LAG_FORWARD, body, 0)

    def drain(c, carry):
        for o in range(n):
            @pl.when(o > z)
            def _():
                send_sum(acc, c, o, True).wait_send()

            @pl.when(o < z)
            def _():
                send_sum(acc, c, o, False).wait_send()

            @pl.when(jnp.logical_and(o <= z, has_right))
            def _():
                send_new(c, o, True).wait_send()

            @pl.when(jnp.logical_and(o >= z, has_left))
            def _():
                send_new(c, o, False).wait_send()

        return carry

    lax.fori_loop(0, chunks, drain, 0)


def outer_step(stepped, outer_params, outer_momentum):
    n = lax.axis_size("rep")
    rows, block = outer_params.shape
    chunks = max(c for c in range(1, 15) if rows % (16 * c) == 0)
    vmem = pl.BlockSpec(memory_space=pltpu.VMEM)
    dma = pltpu.SemaphoreType.DMA((chunks, n))
    return pl.pallas_call(
        functools.partial(outer_kernel, n, chunks),
        out_shape=(
            jax.ShapeDtypeStruct(stepped.shape, WIRE),
            jax.ShapeDtypeStruct(outer_params.shape, jnp.float32),
        ),
        in_specs=[vmem] * 3,
        out_specs=(vmem, vmem),
        scratch_shapes=[
            pltpu.VMEM(stepped.shape, WIRE),
            pltpu.VMEM(stepped.shape, WIRE),
            pltpu.VMEM(stepped.shape, WIRE),
            pltpu.VMEM((rows // chunks, block), jnp.float32),
            dma, dma, dma, dma, dma, dma,
        ],
        compiler_params=pltpu.CompilerParams(
            collective_id=0, has_side_effects=True, vmem_limit_bytes=40 * 2**20
        ),
    )(stepped, outer_params, outer_momentum)


def per_device(
    hidden, out_grad, inner_params, first_moment, second_moment, outer_params, outer_momentum
):
    columns = lax.all_to_all(hidden, "fsdp", split_axis=1, concat_axis=0, tiled=True)
    segment = lax.all_gather(out_grad, "fsdp", axis=0, tiled=True)
    token_count = hidden.shape[0]
    blocks = segment.shape[0] // token_count
    gradient = jnp.einsum(
        "btf,btd->fd",
        columns.reshape(blocks, token_count, columns.shape[1]),
        segment.reshape(blocks, token_count, segment.shape[1]),
        preferred_element_type=jnp.float32,
    )
    stacked = gradient[None]
    moment_one = beta_one * first_moment.astype(jnp.float32) + (1.0 - beta_one) * stacked
    moment_two = beta_two * second_moment.astype(jnp.float32) + (1.0 - beta_two) * stacked * stacked
    corrected_one = moment_one / (1.0 - beta_one**INNER_STEP)
    corrected_two = moment_two / (1.0 - beta_two**INNER_STEP)
    stepped = inner_params - inner_rate * (
        corrected_one / (jnp.sqrt(corrected_two) + epsilon) + weight_decay * inner_params
    )
    gathered, new_momentum = outer_step(stepped[0], outer_params, outer_momentum)
    return (
        gathered.astype(jnp.float32),
        new_momentum,
        moment_one.astype(jnp.bfloat16),
        moment_two.astype(jnp.bfloat16),
    )


def solution(mesh):
    return jax.shard_map(
        per_device,
        mesh=mesh,
        in_specs=(
            P(("rep", "fsdp"), None),
            P(("rep", "fsdp"), None),
            P("rep", "fsdp", None),
            P("rep", "fsdp", None),
            P("rep", "fsdp", None),
            P("fsdp", "rep"),
            P("fsdp", "rep"),
        ),
        out_specs=(
            P("fsdp", None),
            P("fsdp", "rep"),
            P("rep", "fsdp", None),
            P("rep", "fsdp", None),
        ),
        check_vma=False,
    )
```

time: 422 us -> 328 us (0.78)
  waiting for transfers between devices: 278 us -> 16.1 us
  Pallas kernels: 0 us -> 197 us
  other arithmetic: 31.8 us -> 3.99 us
  local copies, waits for them, and re-layouts: 13 us -> 7.15 us
  matrix products: 16.7 us -> 21.9 us
    pallas_call x0 -> x1, Pallas kernels: none -> 197 us  [outer_step(): pl.pallas_call(functools.partial(outer_kernel, n, chunks), out_shape=(jax...]
    all_gather x1 -> x0, waiting for transfers between devices: 133 us -> none  [per_device(): gathered = lax.all_gather(updated, 'rep', axis=1, tiled=True)]
    reduce_scatter x1 -> x0, waiting for transfers between devices: 129 us -> none  [per_device(): lax.psum_scatter(stepped[0], 'rep', scatter_dimension=1, tiled=True)]
    reduce_sum x1 -> x0, other arithmetic: 13.6 us -> none  [per_device(): gradient = jnp.sum(rounded, axis=0)]
    convert_element_type x1, other arithmetic: 13.6 us -> 3.99 us  [per_device(): gathered.astype(jnp.float32)]
    unnamed x4 -> x6, local copies, waits for them, and re-layouts: 13 us -> 7.15 us
    dot_general x1, matrix products: 16.7 us -> 21.9 us  [per_device(): jnp.einsum('btf,btd->fd', columns.reshape(blocks, token_count, columns.sh...]
    sub x1 -> x0, other arithmetic: 4.57 us -> none  [per_device(): outer_params - outer_rate * (outer_delta + nesterov * new_momentum)]
  transfers between devices with their start and end apart: 3 -> 1, of which waited for: 3 -> 1; matrix products, arithmetic and copies ran while one was open for 1% -> 2% of each run, Pallas kernels for 0% -> 0%
where the time goes in v1:
time: 328 us
  Pallas kernels  197 us (60%)
  blocking collectives  68 us (21%)
  matrix products  21.9 us (7%)
  waiting for transfers between devices  16.1 us (5%)
  between operations  14 us (4%)
  local copies, waits for them, and re-layouts  7.15 us (2%)
  other arithmetic  3.99 us (1%)
    pallas_call x1, Pallas kernels, outer_step(): pl.pallas_call(functools.partial(outer_kernel, n, chunks), out_shape=(jax...  197 us
    all_to_all x1, blocking collectives, per_device(): lax.all_to_all(hidden, 'fsdp', split_axis=1, concat_axis=0, tiled=True)  68 us
    dot_general x1, matrix products, per_device(): jnp.einsum('btf,btd->fd', columns.reshape(blocks, token_count, columns.sh...  21.9 us
    all_gather x1, waiting for transfers between devices, per_device(): segment = lax.all_gather(out_grad, 'fsdp', axis=0, tiled=True)  15.4 us
    unnamed x6, local copies, waits for them, and re-layouts  7.15 us
  transfers between devices with their start and end apart: 1, of which 1 were waited for; matrix products, arithmetic and copies ran while one was open for 2% of the time, Pallas kernels for 0%

profile of v1, /device:TPU:0, one launch (start us, length us, event | category | flops | bytes accessed | tf_op | source)
XLA Modules:
  0.0 328.0 jit_solution(12263881561545704365)
XLA Ops:
  7.2 0.0 all-gather.2.cloned.1.call-start
  7.2 0.7 all-gather.2.cloned.1.call-update
  7.9 5.9 %copy.11 = bf16[256,7168]{0,1:T(8,128)(2,1)} copy(bf16[256,7168]{1,0:T(8,128)(2,1)} %param.7) | data formatting | bytes 7340032 | tf_op args[0]
  13.8 68.0 %all_to_all.16 = bf16[256,8,896]{0,2,1:T(8,128)(2,1)} all-to-all(bf16[256,8,896]{0,2,1:T(8,128)(2,1)} %bitcast.37), channel_id=1, replica_groups=mesh['rep'=4,'fsdp'=8] {'fsdp'}, dimensions={1} | all-to-all | bytes 7340032 | tf_op jit(solution)/shard_map/all_to_all | solution.py:230
  81.8 15.4 %all-gather.2.cloned.1.call-done = bf16[2048,2048]{1,0:T(8,128)(2,1)} async-done(((bf16[256,2048]{1,0:T(8,128)(2,1)}), bf16[2048,2048]{1,0:T(8,128)(2,1)}) %all-gather.2.cloned.1.call-update) | async-done | bytes 8388624 | tf_op jit(solution)/shard_map/all_gather | solution.py:231
  97.2 0.0 copy-start
  97.2 0.0 copy-start.1
  97.2 21.9 %fusion.5 = (bf16[1,896,2048]{2,1,0:T(8,128)(2,1)}, f32[896,2048]{1,0:T(8,128)}, bf16[1,896,2048]{2,1,0:T(8,128)(2,1)}) fusion(bf16[1,896,2048]{2,1,0:T(8,128)(2,1)} %param.11, f32[1,896,2048]{2,1,0:T(8,128)} %param.9, bf16[1,896,2048]{2,1,0:T(8,128)(2,1)} %param.10, bf16[8,256,2048]{2,1,0:T(8,128)(2,1)} %bitcast.38, bf16[256,8,896]{0,2,1:T(8,128)(2,1)} %all_to_all.16), kind=kOutput, calls=%fused_computation.9 | convolution fusion | flops 7547387904 | bytes 41418752 | tf_op jit(solution)/shard_map/btf,btd->fd/dot_general | solution.py:234
  119.1 0.0 copy-done
  119.1 0.0 copy-done.1
  119.1 196.8 %shard_map.102 = (bf16[896,2048]{1,0:T(8,128)(2,1)S(1)}, f32[896,512]{1,0:T(8,128)S(1)}) custom-call(f32[896,2048]{1,0:T(8,128)} %get-tuple-element.9.step_ref, f32[896,512]{1,0:T(8,128)S(1)} %copy-done, f32[896,512]{1,0:T(8,128)S(1)} %copy-done.1), custom_call_target="tpu_custom_call" | custom-call | tf_op jit(solution)/shard_map/pallas_call | solution.py:206
  316.0 4.0 %convert_element_type.17 = f32[896,2048]{1,0:T(8,128)} convert(bf16[896,2048]{1,0:T(8,128)(2,1)S(1)} %get-tuple-element.6) | non-fusion elementwise | flops 1835008 | bytes 11010048 | tf_op jit(solution)/shard_map/convert_element_type | solution.py:250
  320.0 1.2 copy.13
Async XLA Ops:
  7.2 90.0 %all-gather.2.cloned.1.call-start = ((), (), s32[]{:S(2)}) async-start(), calls=%async_computation.1 | async-start | bytes 9437184 | tf_op jit(solution)/shard_map/all_gather | solution.py:231
  97.2 21.9 %copy-start = (f32[896,512]{1,0:T(8,128)S(1)}, f32[896,512]{1,0:T(8,128)}, u32[]{:S(2)}) copy-start(f32[896,512]{1,0:T(8,128)} %outer_ref.1) | copy-start | bytes 5505028
  97.2 21.9 %copy-start.1 = (f32[896,512]{1,0:T(8,128)S(1)}, f32[896,512]{1,0:T(8,128)}, u32[]{:S(2)}) copy-start(f32[896,512]{1,0:T(8,128)} %mom_ref.1) | copy-start | bytes 5505028
Sparse Core Ops, SparseCore 0:
  9.9 87.3 all-gather.1

commit v2 on v1

--- a/solution.py
+++ b/solution.py
@@ -19,8 +19,6 @@
 
 WIRE = jnp.bfloat16
 WIRE_SCALE = 16.0
-LAG_OWN = 2
-LAG_FORWARD = 4
 
 
 def encode(value):
@@ -133,46 +131,38 @@
         def _():
             send_new(c, z, False).start()
 
-    def forward(c):
+    def within(c, work):
+        @pl.when(jnp.logical_and(c >= 0, c < chunks))
+        def _():
+            work(c)
+
+    def own_lag(o):
+        return jnp.maximum(o, n - 1 - o)
+
+    def forward(t, distance, to_right):
+        o = z - distance if to_right else z + distance
+        there = o >= 0 if to_right else o < n
+        c = t - own_lag(o) - distance
+        ready = jnp.logical_and(there, jnp.logical_and(c >= 0, c < chunks))
+
+        @pl.when(ready)
+        def _():
+            send_new(c, o, to_right).wait_recv()
+
+        @pl.when(jnp.logical_and(ready, has_right if to_right else has_left))
+        def _():
+            send_new(c, o, to_right).start()
+
+    def body(t, carry):
+        within(t - z, lambda c: wave(c, True))
+        within(t - (n - 1 - z), lambda c: wave(c, False))
+        within(t - own_lag(z), own)
         for distance in range(1, n):
-            for to_right in (True, False):
-                o = z - distance if to_right else z + distance
-                there = o >= 0 if to_right else o < n
-
-                @pl.when(there)
-                def _():
-                    send_new(c, o, to_right).wait_recv()
-
-                @pl.when(jnp.logical_and(there, has_right if to_right else has_left))
-                def _():
-                    send_new(c, o, to_right).start()
-
-    def body(t, carry):
-        @pl.when(t < chunks)
-        def _():
-            near_left = z < n // 2
-
-            @pl.when(near_left)
-            def _():
-                wave(t, True)
-                wave(t, False)
-
-            @pl.when(jnp.logical_not(near_left))
-            def _():
-                wave(t, False)
-                wave(t, True)
-
-        @pl.when(jnp.logical_and(t >= LAG_OWN, t < chunks + LAG_OWN))
-        def _():
-            own(t - LAG_OWN)
-
-        @pl.when(t >= LAG_FORWARD)
-        def _():
-            forward(t - LAG_FORWARD)
-
+            forward(t, distance, True)
+            forward(t, distance, False)
         return carry
 
-    lax.fori_loop(0, chunks + LAG_FORWARD, body, 0)
+    lax.fori_loop(0, chunks + 2 * (n - 1), body, 0)
 
     def drain(c, carry):
         for o in range(n):

time: 328 us -> 233 us (0.71)
  Pallas kernels: 197 us -> 102 us
    pallas_call x1, Pallas kernels: 197 us -> 102 us  [outer_step(): pl.pallas_call(functools.partial(outer_kernel, n, chunks), out_shape=(jax...]
  transfers between devices with their start and end apart: 1 -> 1, of which waited for: 1 -> 1; matrix products, arithmetic and copies ran while one was open for 2% -> 3% of each run, Pallas kernels for 0% -> 0%
where the time goes in v2:
time: 233 us
  Pallas kernels  102 us (44%)
  blocking collectives  68 us (29%)
  matrix products  21.9 us (9%)
  waiting for transfers between devices  16.1 us (7%)
  between operations  14 us (6%)
  local copies, waits for them, and re-layouts  7.15 us (3%)
  other arithmetic  3.99 us (2%)
    pallas_call x1, Pallas kernels, outer_step(): pl.pallas_call(functools.partial(outer_kernel, n, chunks), out_shape=(jax...  102 us
    all_to_all x1, blocking collectives, per_device(): lax.all_to_all(hidden, 'fsdp', split_axis=1, concat_axis=0, tiled=True)  68 us
    dot_general x1, matrix products, per_device(): jnp.einsum('btf,btd->fd', columns.reshape(blocks, token_count, columns.sh...  21.9 us
    all_gather x1, waiting for transfers between devices, per_device(): segment = lax.all_gather(out_grad, 'fsdp', axis=0, tiled=True)  15.4 us
    unnamed x6, local copies, waits for them, and re-layouts  7.15 us
  transfers between devices with their start and end apart: 1, of which 1 were waited for; matrix products, arithmetic and copies ran while one was open for 3% of the time, Pallas kernels for 0%

profile of v2, /device:TPU:0, one launch (start us, length us, event | category | flops | bytes accessed | tf_op | source)
XLA Modules:
  0.0 232.9 jit_solution(11387585317660952819)
XLA Ops:
  7.2 0.0 all-gather.2.cloned.1.call-start
  7.2 0.7 all-gather.2.cloned.1.call-update
  7.9 5.9 %copy.11 = bf16[256,7168]{0,1:T(8,128)(2,1)} copy(bf16[256,7168]{1,0:T(8,128)(2,1)} %param.7) | data formatting | bytes 7340032 | tf_op args[0]
  13.8 68.0 %all_to_all.16 = bf16[256,8,896]{0,2,1:T(8,128)(2,1)} all-to-all(bf16[256,8,896]{0,2,1:T(8,128)(2,1)} %bitcast.37), channel_id=1, replica_groups=mesh['rep'=4,'fsdp'=8] {'fsdp'}, dimensions={1} | all-to-all | bytes 7340032 | tf_op jit(solution)/shard_map/all_to_all | solution.py:220
  81.8 15.4 %all-gather.2.cloned.1.call-done = bf16[2048,2048]{1,0:T(8,128)(2,1)} async-done(((bf16[256,2048]{1,0:T(8,128)(2,1)}), bf16[2048,2048]{1,0:T(8,128)(2,1)}) %all-gather.2.cloned.1.call-update) | async-done | bytes 8388624 | tf_op jit(solution)/shard_map/all_gather | solution.py:221
  97.2 0.0 copy-start
  97.2 0.0 copy-start.1
  97.2 21.9 %fusion.5 = (bf16[1,896,2048]{2,1,0:T(8,128)(2,1)}, f32[896,2048]{1,0:T(8,128)}, bf16[1,896,2048]{2,1,0:T(8,128)(2,1)}) fusion(bf16[1,896,2048]{2,1,0:T(8,128)(2,1)} %param.11, f32[1,896,2048]{2,1,0:T(8,128)} %param.9, bf16[1,896,2048]{2,1,0:T(8,128)(2,1)} %param.10, bf16[8,256,2048]{2,1,0:T(8,128)(2,1)} %bitcast.38, bf16[256,8,896]{0,2,1:T(8,128)(2,1)} %all_to_all.16), kind=kOutput, calls=%fused_computation.9 | convolution fusion | flops 7547387904 | bytes 41418752 | tf_op jit(solution)/shard_map/btf,btd->fd/dot_general | solution.py:224
  119.1 0.0 copy-done
  119.1 0.0 copy-done.1
  119.1 101.7 %shard_map.102 = (bf16[896,2048]{1,0:T(8,128)(2,1)S(1)}, f32[896,512]{1,0:T(8,128)S(1)}) custom-call(f32[896,2048]{1,0:T(8,128)} %get-tuple-element.9.step_ref, f32[896,512]{1,0:T(8,128)S(1)} %copy-done, f32[896,512]{1,0:T(8,128)S(1)} %copy-done.1), custom_call_target="tpu_custom_call" | custom-call | tf_op jit(solution)/shard_map/pallas_call | solution.py:196
  220.9 4.0 %convert_element_type.17 = f32[896,2048]{1,0:T(8,128)} convert(bf16[896,2048]{1,0:T(8,128)(2,1)S(1)} %get-tuple-element.6) | non-fusion elementwise | flops 1835008 | bytes 11010048 | tf_op jit(solution)/shard_map/convert_element_type | solution.py:240
  224.9 1.2 copy.13
Async XLA Ops:
  7.2 90.0 %all-gather.2.cloned.1.call-start = ((), (), s32[]{:S(2)}) async-start(), calls=%async_computation.1 | async-start | bytes 9437184 | tf_op jit(solution)/shard_map/all_gather | solution.py:221
  97.2 21.9 %copy-start = (f32[896,512]{1,0:T(8,128)S(1)}, f32[896,512]{1,0:T(8,128)}, u32[]{:S(2)}) copy-start(f32[896,512]{1,0:T(8,128)} %outer_ref.1) | copy-start | bytes 5505028
  97.2 21.9 %copy-start.1 = (f32[896,512]{1,0:T(8,128)S(1)}, f32[896,512]{1,0:T(8,128)}, u32[]{:S(2)}) copy-start(f32[896,512]{1,0:T(8,128)} %mom_ref.1) | copy-start | bytes 5505028
Sparse Core Ops, SparseCore 0:
  9.9 87.3 all-gather.1
